TPU v7x, 32 devices: a whole 2x2x4 slice. The times are simulated.
32 devices in a mesh: sib: 4 (over y, x), wide: 8 (over z, core).
Axes of the slice: x: 2, y: 2, z: 4, core: 2. Of those that a mesh axis runs over, the one named last changes fastest.
Arguments:
- right_side: float32 [128, 8, 2048], P(None, 'wide', 'sib'), may hold values from -6 to 6
- tree_order: int32 [8, 2048], P('wide', 'sib'), may hold values from 0 to 2047, each once within a row
- x_start: float32 [128, 8, 2048], P(None, 'wide', 'sib'), may hold values from -6 to 6
- tangent_start: float32 [128, 8, 2048], P(None, 'wide', 'sib'), may hold values from -3 to 3
- dense_kernel: float32 [8, 4, 512, 512], P('wide', 'sib'), may hold values from -0.25 to 0.25
- dense_deriv: float32 [8, 4, 512, 512], P('wide', 'sib'), may hold values from -0.25 to 0.25
- leaf_basis: float32 [8, 4, 512, 256], P('wide', 'sib'), may hold values from -0.25 to 0.25
- transfer: float32 [8, 4, 256, 256], P('wide', 'sib'), may hold values from -0.375 to 0.375
- sibling_kernel: float32 [8, 4, 3, 256, 256], P('wide', 'sib'), may hold values from -0.21875 to 0.21875
- sibling_deriv: float32 [8, 4, 3, 256, 256], P('wide', 'sib'), may hold values from -0.21875 to 0.21875
- partner_list: int32 [8, 4], P('wide'), may hold values from 0 to 7, as said below
- parent_kernel: float32 [8, 4, 256, 256], P('wide'), may hold values from -0.1875 to 0.1875
- parent_deriv: float32 [8, 4, 256, 256], P('wide'), may hold values from -0.1875 to 0.1875
Outputs:
- solution: float32 [128, 8, 2048], P(None, 'wide', 'sib')
- tangent: float32 [128, 8, 2048], P(None, 'wide', 'sib')
Inputs may be any that keep to these rules, and one draw needn't show every extreme that they name: `partner_list`: row p names 4 different parent clusters, none of them p. `tree_order`: each row holds every position 0 .. 2047 once.
All inputs are finite; a program needn't handle non-finite values.
Results may differ from a plain program's by a relative error of at most 0.0001.
Values sent between devices are 32-bit elements; how exact they have to be, the bound alone decides.
No kernel may reach another device: no remote copies, remote signals or barrier semaphores. Data moves between devices by JAX's collectives and lax.ppermute only.
A program may use at most 64 MiB of HBM per device.

v0:
```python
import jax
import jax.numpy as jnp
from jax import lax
from jax.sharding import PartitionSpec as P

ITERS = 2
highest = lax.Precision.HIGHEST
relax_step = 0.3
noise_level = 1.0


def product(left, right):
    return jnp.dot(left, right, precision=highest, preferred_element_type=jnp.float32)


def product_t(left, right):
    return lax.dot_general(
        left, right, (((1,), (1,)), ((), ())), precision=highest, preferred_element_type=jnp.float32
    )


def body(
    right_side,
    tree_order,
    x_start,
    tangent_start,
    dense_kernel,
    dense_deriv,
    leaf_basis,
    transfer,
    sibling_kernel,
    sibling_deriv,
    partner_list,
    parent_kernel,
    parent_deriv,
):
    order = tree_order[0]
    dense = dense_kernel[0, 0]
    dense_d = dense_deriv[0, 0]
    basis = leaf_basis[0, 0]
    trans = transfer[0, 0]
    sib_k = sibling_kernel[0, 0]
    sib_d = sibling_deriv[0, 0]
    partners = partner_list[0]
    par_k = parent_kernel[0]
    par_d = parent_deriv[0]
    me = lax.axis_index("sib")
    count = lax.axis_size("sib")
    piece = lax.all_gather(right_side, "sib", axis=2, tiled=True)
    rows = piece.shape[2]
    inside = (order >= 0) & (order < rows)
    taken = jnp.take(piece[:, 0, :], jnp.clip(order, 0, rows - 1), axis=1)
    rhs = jnp.where(inside[None, :], taken, 0.0)
    x = x_start[:, 0, :]
    dx = tangent_start[:, 0, :]
    for step in range(ITERS):
        coeff_x = product(x, basis)
        coeff_dx = product(dx, basis)
        empty = jnp.zeros(coeff_x.shape, jnp.float32)
        term_x = product(coeff_x, trans)
        term_dx = product(coeff_dx, trans)
        start = jnp.int32(0)
        add_field_x = empty
        add_field_dx = empty
        add_piece_x = lax.all_gather(coeff_x[None], "sib", axis=0, tiled=True)
        add_piece_dx = lax.all_gather(coeff_dx[None], "sib", axis=0, tiled=True)
        for item in range(add_piece_x.shape[0]):
            other = start + item
            slot = jnp.clip((other - me - 1 + count) % count, 0, count - 2)
            weight = jnp.where(other == me, 0.0, 1.0).astype(jnp.float32)
            kern = lax.dynamic_index_in_dim(sib_k, slot, 0, keepdims=False)
            deriv = lax.dynamic_index_in_dim(sib_d, slot, 0, keepdims=False)
            add_field_x = add_field_x + weight * product(add_piece_x[item], kern)
            add_field_dx = add_field_dx + weight * (
                product(add_piece_x[item], deriv) + product(add_piece_dx[item], kern)
            )
        upper_x, upper_dx = (
            lax.psum_scatter(term_x, "sib", scatter_dimension=0, tiled=True),
            lax.psum_scatter(term_dx, "sib", scatter_dimension=0, tiled=True),
        )
        piece_x = lax.all_gather(upper_x[None], "wide", axis=0, tiled=True)
        piece_dx = lax.all_gather(upper_dx[None], "wide", axis=0, tiled=True)
        index = jnp.arange(piece_x.shape[0], dtype=jnp.int32)
        select = (index[None, :] == partners[:, None]).astype(jnp.float32)
        chosen_x = jnp.einsum(
            "bn,nrk->brk", select, piece_x, precision=highest, preferred_element_type=jnp.float32
        )
        chosen_dx = jnp.einsum(
            "bn,nrk->brk", select, piece_dx, precision=highest, preferred_element_type=jnp.float32
        )
        field_x = jnp.einsum(
            "brk,bkm->rm", chosen_x, par_k, precision=highest, preferred_element_type=jnp.float32
        )
        field_dx = jnp.einsum(
            "brk,bkm->rm", chosen_x, par_d, precision=highest, preferred_element_type=jnp.float32
        ) + jnp.einsum(
            "brk,bkm->rm", chosen_dx, par_k, precision=highest, preferred_element_type=jnp.float32
        )
        far_x, far_dx = (
            lax.all_gather(field_x, "sib", axis=0, tiled=True),
            lax.all_gather(field_dx, "sib", axis=0, tiled=True),
        )
        down_x = add_field_x + product_t(far_x, trans)
        down_dx = add_field_dx + product_t(far_dx, trans)
        image = product(x, dense) + product_t(down_x, basis)
        dimage = product(x, dense_d) + product(dx, dense) + product_t(down_dx, basis)
        x_next = x + relax_step * (rhs - noise_level * x - image)
        dx = dx - relax_step * (noise_level * dx + dimage)
        x = x_next
    return (x[:, None, :], dx[:, None, :])


def solution(mesh):
    placed = (
        P(None, "wide", "sib"),
        P("wide", "sib"),
        P(None, "wide", "sib"),
        P(None, "wide", "sib"),
        P("wide", "sib", None, None),
        P("wide", "sib", None, None),
        P("wide", "sib", None, None),
        P("wide", "sib", None, None),
        P("wide", "sib", None, None, None),
        P("wide", "sib", None, None, None),
        P("wide", None),
        P("wide", None, None, None),
        P("wide", None, None, None),
    )
    return jax.shard_map(
        body,
        mesh=mesh,
        in_specs=placed,
        out_specs=(P(None, "wide", "sib"), P(None, "wide", "sib")),
        check_vma=False,
    )
```

profile of v0, /device:TPU:0, one launch (start us, length us, event | category | flops | bytes accessed | tf_op | source)
XLA Modules:
  0.0 240.8 jit_solution(12168629055974303689)
XLA Ops:
  7.2 1.6 fusion.62
  8.9 0.9 fusion.95
  10.3 0.9 fusion.89
  11.4 12.0 %all-gather = f32[512,256]{1,0:T(8,128)S(1)} all-gather(f32[128,256]{1,0:T(8,128)S(1)} %fusion.62), channel_id=2, replica_groups=mesh['sib'=4,'wide'=8] {'sib'}, dimensions={0}, use_global_device_ids=true | all-gather | bytes 655360 | tf_op jit(solution)/shard_map/all_gather | solution.py:65
  23.4 11.2 %all-gather.4 = f32[512,256]{1,0:T(8,128)} all-gather(f32[128,256]{1,0:T(8,128)S(1)} %fusion.56), channel_id=6, replica_groups=mesh['sib'=4,'wide'=8] {'sib'}, dimensions={0}, use_global_device_ids=true | all-gather | bytes 655360 | tf_op jit(solution)/shard_map/all_gather | solution.py:66
  34.9 0.9 fusion.79
  35.8 0.9 fusion.75
  36.8 0.9 fusion.71
  37.7 2.0 fusion.40
  39.7 1.4 convolution_add_fusion.5
  43.9 0.9 fusion.22
  44.8 14.7 %all-gather.1 = f32[256,256]{1,0:T(8,128)S(1)} all-gather(f32[32,256]{1,0:T(8,128)} %reduce-scatter.5.cloned.1.call-done), channel_id=3, replica_groups=mesh['sib'=4,'wide'=8] {'wide'}, dimensions={0}, use_global_device_ids=true | all-gather | bytes 294912 | tf_op jit(solution)/shard_map/all_gather | solution.py:81
  59.5 0.7 copy-done.34
  60.6 4.5 %reduce-scatter.9.cloned.1.call-done = f32[32,256]{1,0:T(8,128)} async-done(((f32[128,256]{1,0:T(8,128)}), f32[32,256]{1,0:T(8,128)}) %reduce-scatter.9.cloned.1.call-update) | async-done | bytes 32784 | tf_op jit(solution)/shard_map/reduce_scatter | solution.py:79
  65.2 14.6 %all-gather.5 = f32[256,256]{1,0:T(8,128)S(1)} all-gather(f32[32,256]{1,0:T(8,128)} %reduce-scatter.9.cloned.1.call-done), channel_id=7, replica_groups=mesh['sib'=4,'wide'=8] {'wide'}, dimensions={0}, use_global_device_ids=true | all-gather | bytes 294912 | tf_op jit(solution)/shard_map/all_gather | solution.py:82
  80.1 1.8 convolution_bitcast_fusion.3
  82.6 8.6 %all_gather.48 = f32[128,256]{1,0:T(8,128)S(1)} all-gather(f32[32,256]{1,0:T(8,128)S(1)} %fusion.35), channel_id=1, replica_groups=mesh['sib'=4,'wide'=8] {'sib'}, dimensions={0}, use_global_device_ids=true | all-gather | bytes 163840 | tf_op jit(solution)/shard_map/all_gather | solution.py:101
  92.2 0.6 fusion.8
  93.6 0.6 copy-done.20
  94.2 0.9 fusion.86
  95.2 1.8 copy.21
  98.7 1.4 fusion.50
  100.7 7.8 %all_gather.42 = f32[128,256]{1,0:T(8,128)S(1)} all-gather(f32[32,256]{1,0:T(8,128)S(1)} %convolution_bitcast_fusion.5), channel_id=1, replica_groups=mesh['sib'=4,'wide'=8] {'sib'}, dimensions={0}, use_global_device_ids=true | all-gather | bytes 163840 | tf_op jit(solution)/shard_map/all_gather | solution.py:100
  108.5 10.8 %all-gather.6 = f32[512,256]{1,0:T(8,128)} all-gather(f32[128,256]{1,0:T(8,128)S(1)} %copy-done.21), channel_id=8, replica_groups=mesh['sib'=4,'wide'=8] {'sib'}, dimensions={0}, use_global_device_ids=true | all-gather | bytes 655360 | tf_op jit(solution)/shard_map/all_gather | solution.py:66
  119.7 14.5 %all-gather.7 = f32[256,256]{1,0:T(8,128)S(1)} all-gather(f32[32,256]{1,0:T(8,128)} %reduce-scatter.11.cloned.1.call-done), channel_id=9, replica_groups=mesh['sib'=4,'wide'=8] {'wide'}, dimensions={0}, use_global_device_ids=true | all-gather | bytes 294912 | tf_op jit(solution)/shard_map/all_gather | solution.py:82
  134.2 1.1 fusion.113
  135.3 13.0 %all-gather.10.cloned.1.call-done = f32[128,1,2048]{0,2,1:T(8,128)} async-done(((f32[128,1,512]{0,2,1:T(8,128)}), f32[128,1,2048]{0,2,1:T(8,128)}) %all-gather.10.cloned.1.call-update) | async-done | bytes 1048592 | tf_op jit(solution)/shard_map/all_gather | solution.py:49
  148.3 2.3 gather_fusion
  150.7 1.7 fusion.13
  152.8 0.9 fusion.92
  153.7 10.2 %all-gather.2 = f32[512,256]{1,0:T(8,128)S(1)} all-gather(f32[128,256]{1,0:T(8,128)S(1)} %fusion.59), channel_id=4, replica_groups=mesh['sib'=4,'wide'=8] {'sib'}, dimensions={0}, use_global_device_ids=true | all-gather | bytes 655360 | tf_op jit(solution)/shard_map/all_gather | solution.py:65
  163.9 2.0 fusion.81
  165.9 0.9 fusion.77
  166.8 0.9 fusion.73
  167.8 0.9 fusion.69
  168.7 1.4 fusion.38
  170.4 2.5 %convolution_add_fusion.4 = f32[128,512]{1,0:T(8,128)} fusion(f32[128,512]{1,0:T(8,128)} %fusion.38, f32[128,512]{1,0:T(8,128)} %copy-done.10, f32[1,1,512,512]{3,2,1,0:T(8,128)S(1)} %copy-done), kind=kOutput, calls=%fused_computation.19 | convolution fusion | flops 402718720 | bytes 1835008 | tf_op jit(solution)/shard_map/dot_general | solution.py:13
  176.6 0.6 copy-done.27
  177.5 0.7 fusion.48
  178.2 16.5 %reduce-scatter.7.cloned.1.call-done = f32[32,256]{1,0:T(8,128)} async-done(((f32[128,256]{1,0:T(8,128)}), f32[32,256]{1,0:T(8,128)}) %reduce-scatter.7.cloned.1.call-update) | async-done | bytes 32784 | tf_op jit(solution)/shard_map/reduce_scatter | solution.py:78
  194.7 14.6 %all-gather.3 = f32[256,256]{1,0:T(8,128)S(1)} all-gather(f32[32,256]{1,0:T(8,128)} %reduce-scatter.7.cloned.1.call-done), channel_id=5, replica_groups=mesh['sib'=4,'wide'=8] {'wide'}, dimensions={0}, use_global_device_ids=true | all-gather | bytes 294912 | tf_op jit(solution)/shard_map/all_gather | solution.py:81
  209.7 1.8 convolution_bitcast_fusion.1
  213.1 8.4 %all_gather.51 = f32[128,256]{1,0:T(8,128)S(1)} all-gather(f32[32,256]{1,0:T(8,128)S(1)} %fusion.34), channel_id=1, replica_groups=mesh['sib'=4,'wide'=8] {'sib'}, dimensions={0}, use_global_device_ids=true | all-gather | bytes 163840 | tf_op jit(solution)/shard_map/all_gather | solution.py:101
  222.5 0.6 fusion.6
  223.2 1.0 copy.26
  224.1 7.5 %all_gather.45 = f32[128,256]{1,0:T(8,128)S(1)} all-gather(f32[32,256]{1,0:T(8,128)S(1)} %convolution_bitcast_fusion.4), channel_id=1, replica_groups=mesh['sib'=4,'wide'=8] {'sib'}, dimensions={0}, use_global_device_ids=true | all-gather | bytes 163840 | tf_op jit(solution)/shard_map/all_gather | solution.py:100
  232.6 0.7 fusion.11
  233.3 1.0 copy.25
  (115 shorter events, 18.0 us)
Async XLA Ops:
  7.2 32.5 %copy-start = (f32[1,1,512,512]{3,2,1,0:T(8,128)S(1)}, f32[1,1,512,512]{3,2,1,0:T(8,128)}, u32[]{:S(2)}) copy-start(f32[1,1,512,512]{3,2,1,0:T(8,128)} %param.17) | copy-start | bytes 3145732
  7.2 1.7 copy-start.3
  7.2 37.6 %reduce-scatter.5.cloned.1.call-start = ((), (), s32[]{:S(2)}) async-start(), calls=%async_computation.5 | async-start | bytes 163840 | tf_op jit(solution)/shard_map/reduce_scatter | solution.py:78
  7.2 2.7 %copy-start.13 = (f32[128,1,512]{2,1,0:T(1,128)S(1)}, f32[128,1,512]{2,1,0:T(1,128)}, u32[]{:S(2)}) copy-start(f32[128,1,512]{2,1,0:T(1,128)} %param.16) | copy-start | bytes 786436
  8.9 1.0 copy-start.1
  9.9 55.3 %reduce-scatter.9.cloned.1.call-start = ((), (), s32[]{:S(2)}) async-start(), calls=%async_computation.7 | async-start | bytes 163840 | tf_op jit(solution)/shard_map/reduce_scatter | solution.py:79
  11.3 23.3 %copy-start.7 = (f32[1,1,3,256,256]{4,3,2,1,0:T(8,128)S(1)}, f32[1,1,3,256,256]{4,3,2,1,0:T(8,128)}, u32[]{:S(2)}) copy-start(f32[1,1,3,256,256]{4,3,2,1,0:T(8,128)} %param.22) | copy-start | bytes 2359300
  11.3 108.4 %reduce-scatter.11.cloned.1.call-start = ((), (), s32[]{:S(2)}) async-start(), calls=%async_computation.8 | async-start | bytes 163840 | tf_op jit(solution)/shard_map/reduce_scatter | solution.py:79
  36.7 1.0 copy-start.12
  37.7 2.0 copy-start.14
  39.7 1.4 copy-start.2
  39.7 1.4 copy-start.18
  41.2 0.9 copy-start.26
  42.1 0.9 copy-start.29
  43.0 0.9 copy-start.32
  59.5 0.7 copy-start.34
  65.2 16.8 %copy-start.4 = (f32[1,4,256,256]{3,2,1,0:T(8,128)S(1)}, f32[1,4,256,256]{3,2,1,0:T(8,128)}, u32[]{:S(2)}) copy-start(f32[1,4,256,256]{3,2,1,0:T(8,128)} %param.24) | copy-start | bytes 3145732
  82.6 8.6 %copy-start.30 = (f32[128,256]{1,0:T(8,128)S(1)}, f32[128,256]{1,0:T(8,128)}, u32[]{:S(2)}) copy-start(f32[128,256]{1,0:T(8,128)} %fusion.22) | copy-start | bytes 393220
  91.2 1.0 copy-start.15
  91.2 1.0 copy-start.23
  92.8 0.7 copy-start.10
  93.6 0.6 copy-start.20
  95.2 53.1 %all-gather.10.cloned.1.call-start = ((), (), s32[]{:S(2)}) async-start(), calls=%async_computation.4 | async-start | bytes 1310720 | tf_op jit(solution)/shard_map/all_gather | solution.py:49
  97.0 0.7 copy-start.33
  97.0 97.7 %reduce-scatter.7.cloned.1.call-start = ((), (), s32[]{:S(2)}) async-start(), calls=%async_computation.6 | async-start | bytes 163840 | tf_op jit(solution)/shard_map/reduce_scatter | solution.py:78
  98.4 1.7 copy-start.5
  100.7 7.8 %copy-start.21 = (f32[128,256]{1,0:T(8,128)S(1)}, f32[128,256]{1,0:T(8,128)}, u32[]{:S(2)}) copy-start(f32[128,256]{1,0:T(8,128)} %copy-done.20) | copy-start | bytes 393220
  150.7 1.7 copy-start.16
  153.7 12.2 %copy-start.8 = (f32[1,1,3,256,256]{4,3,2,1,0:T(8,128)S(1)}, f32[1,1,3,256,256]{4,3,2,1,0:T(8,128)}, u32[]{:S(2)}) copy-start(f32[1,1,3,256,256]{4,3,2,1,0:T(8,128)} %param.22) | copy-start | bytes 2359300
  163.9 4.8 %copy-start.9 = (f32[1,1,512,512]{3,2,1,0:T(8,128)S(1)}, f32[1,1,512,512]{3,2,1,0:T(8,128)}, u32[]{:S(2)}) copy-start(f32[1,1,512,512]{3,2,1,0:T(8,128)} %param.18) | copy-start | bytes 3145732
  173.2 1.0 copy-start.19
  173.5 0.9 copy-start.24
  174.5 0.9 copy-start.31
  175.4 0.9 copy-start.28
  176.3 0.9 copy-start.27
  194.7 16.8 %copy-start.6 = (f32[1,4,256,256]{3,2,1,0:T(8,128)S(1)}, f32[1,4,256,256]{3,2,1,0:T(8,128)}, u32[]{:S(2)}) copy-start(f32[1,4,256,256]{3,2,1,0:T(8,128)} %param.24) | copy-start | bytes 3145732
  211.6 0.9 copy-start.25
  221.5 1.0 copy-start.11
  221.5 1.0 copy-start.22
  231.7 1.0 copy-start.17
Sparse Core Ops, SparseCore 0:
  11.3 26.8 reduce-scatter.4
  41.0 24.1 reduce-scatter.8
  95.3 24.0 reduce-scatter.10
  121.7 26.5 all-gather.9
  170.6 24.1 reduce-scatter.6
where the time goes:
time: 242 us; the launch traced here: 241 us
  blocking collectives  135 us (56%)
  matrix products  42.6 us (18%)
  waiting for transfers between devices  34.2 us (14%)
  local copies, waits for them, and re-layouts  14.5 us (6%)
  between operations  14.4 us (6%)
    all_gather x2, blocking collectives, body(): piece_x = lax.all_gather(upper_x[None], 'wide', axis=0, tiled=True)  29.3 us
    dot_general x38, matrix products, product(): jnp.dot(left, right, precision=highest, preferred_element_type=jnp.float32)  29.1 us
    all_gather x2, blocking collectives, body(): piece_dx = lax.all_gather(upper_dx[None], 'wide', axis=0, tiled=True)  29.1 us
    all_gather x2, blocking collectives, body(): add_piece_x = lax.all_gather(coeff_x[None], 'sib', axis=0, tiled=True)  22.2 us
    all_gather x2, blocking collectives, body(): add_piece_dx = lax.all_gather(coeff_dx[None], 'sib', axis=0, tiled=True)  22 us
    all_gather x2, blocking collectives, body(): lax.all_gather(field_dx, 'sib', axis=0, tiled=True)  17 us
    reduce_scatter x2, waiting for transfers between devices, body(): lax.psum_scatter(term_x, 'sib', scatter_dimension=0, tiled=True)  16.5 us
    all_gather x2, blocking collectives, body(): lax.all_gather(field_x, 'sib', axis=0, tiled=True)  15.3 us
  transfers between devices with their start and end apart: 5, of which 3 were waited for; matrix products, arithmetic and copies ran while one was open for 9% of the time, Pallas kernels for 0%

commit v1 on v0

--- a/solution.py
+++ b/solution.py
@@ -7,6 +7,22 @@
 highest = lax.Precision.HIGHEST
 relax_step = 0.3
 noise_level = 1.0
+
+
+def product_in_turn(x, axis, dim, product):
+    devices, index, rows = (lax.axis_size(axis), lax.axis_index(axis), x.shape[dim])
+    right = [(i, (i + 1) % devices) for i in range(devices)]
+    downward = [(i, (i - 1) % devices) for i in range(devices)]
+    half = devices // 2
+    from_left = from_right = x
+    total = product(x, index * rows)
+    for lap in range(1, half + 1):
+        from_left = lax.ppermute(from_left, axis, right)
+        if lap < devices - half:
+            from_right = lax.ppermute(from_right, axis, downward)
+            total = total + product(from_right, (index + lap) % devices * rows)
+        total = total + product(from_left, (index - lap) % devices * rows)
+    return total
 
 
 def product(left, right):
@@ -79,14 +95,22 @@
             lax.psum_scatter(term_dx, "sib", scatter_dimension=0, tiled=True),
         )
         piece_x = lax.all_gather(upper_x[None], "wide", axis=0, tiled=True)
-        piece_dx = lax.all_gather(upper_dx[None], "wide", axis=0, tiled=True)
         index = jnp.arange(piece_x.shape[0], dtype=jnp.int32)
         select = (index[None, :] == partners[:, None]).astype(jnp.float32)
         chosen_x = jnp.einsum(
             "bn,nrk->brk", select, piece_x, precision=highest, preferred_element_type=jnp.float32
         )
-        chosen_dx = jnp.einsum(
-            "bn,nrk->brk", select, piece_dx, precision=highest, preferred_element_type=jnp.float32
+        chosen_dx = product_in_turn(
+            upper_dx[None],
+            "wide",
+            0,
+            lambda part, offset: jnp.einsum(
+                "bn,nrk->brk",
+                lax.dynamic_slice_in_dim(select, offset, part.shape[0], axis=1),
+                part,
+                precision=highest,
+                preferred_element_type=jnp.float32,
+            ),
         )
         field_x = jnp.einsum(
             "brk,bkm->rm", chosen_x, par_k, precision=highest, preferred_element_type=jnp.float32

time: 242 us -> 257 us (1.062)
  blocking collectives: 135 us -> 109 us
  starting transfers between devices: 0.21 us -> 17.1 us
  waiting for transfers between devices: 34.2 us -> 49.9 us
  matrix products: 42.6 us -> 47.1 us
    all_gather x2 -> x0, blocking collectives: 29.1 us -> none  [body(): piece_dx = lax.all_gather(upper_dx[None], 'wide', axis=0, tiled=True)]
    ppermute x0 -> x14, starting transfers between devices: none -> 16.9 us  [the longest x6 16.9 us: product_in_turn(): from_right = lax.ppermute(from_right, axis, downward)]
    all_gather x1, waiting for transfers between devices: 13 us -> 0.01 us  [body(): piece = lax.all_gather(right_side, 'sib', axis=2, tiled=True)]
    reduce_scatter x2, waiting for transfers between devices: 16.5 us -> 28.4 us  [body(): lax.psum_scatter(term_x, 'sib', scatter_dimension=0, tiled=True)]
    reduce_scatter x2, waiting for transfers between devices: 4.57 us -> 14.8 us  [body(): lax.psum_scatter(term_dx, 'sib', scatter_dimension=0, tiled=True)]
    ppermute x0 -> x14, waiting for transfers between devices: none -> 6.62 us  [the longest x8 4.79 us: product_in_turn(): from_left = lax.ppermute(from_left, axis, right)]
    unnamed x73 -> x125, local copies, waits for them, and re-layouts: 12.1 us -> 13.7 us
  transfers between devices with their start and end apart: 5 -> 19, of which waited for: 3 -> 8; matrix products, arithmetic and copies ran while one was open for 9% -> 17% of each run, Pallas kernels for 0% -> 0%
where the time goes in v1:
time: 257 us; the launch traced here: 256 us
  blocking collectives  109 us (42%)
  waiting for transfers between devices  49.9 us (19%)
  matrix products  47.1 us (18%)
  starting transfers between devices  17.1 us (7%)
  local copies, waits for them, and re-layouts  16.8 us (7%)
  between operations  14.7 us (6%)
    dot_general x38, matrix products, product(): jnp.dot(left, right, precision=highest, preferred_element_type=jnp.float32)  31.5 us
    all_gather x2, blocking collectives, body(): piece_x = lax.all_gather(upper_x[None], 'wide', axis=0, tiled=True)  29.1 us
    reduce_scatter x2, waiting for transfers between devices, body(): lax.psum_scatter(term_x, 'sib', scatter_dimension=0, tiled=True)  28.4 us
    all_gather x2, blocking collectives, body(): add_piece_dx = lax.all_gather(coeff_dx[None], 'sib', axis=0, tiled=True)  23.8 us
    all_gather x2, blocking collectives, body(): add_piece_x = lax.all_gather(coeff_x[None], 'sib', axis=0, tiled=True)  22.8 us
    all_gather x2, blocking collectives, body(): lax.all_gather(field_dx, 'sib', axis=0, tiled=True)  17.1 us
    ppermute x6, starting transfers between devices, product_in_turn(): from_right = lax.ppermute(from_right, axis, downward)  16.9 us
    all_gather x2, blocking collectives, body(): lax.all_gather(field_x, 'sib', axis=0, tiled=True)  16.2 us
  transfers between devices with their start and end apart: 19, of which 8 were waited for; matrix products, arithmetic and copies ran while one was open for 17% of the time, Pallas kernels for 0%

profile of v1, /device:TPU:0, one launch (start us, length us, event | category | flops | bytes accessed | tf_op | source)
XLA Modules:
  0.0 256.3 jit_solution(2117172351519161854)
XLA Ops:
  7.2 1.6 fusion.56
  12.2 12.3 %all-gather = f32[512,256]{1,0:T(8,128)S(1)} all-gather(f32[128,256]{1,0:T(8,128)} %copy-done.18), channel_id=2, replica_groups=mesh['sib'=4,'wide'=8] {'sib'}, dimensions={0}, use_global_device_ids=true | all-gather | bytes 655360 | tf_op jit(solution)/shard_map/all_gather | solution.py:81
  24.5 10.2 %all-gather.4 = f32[512,256]{1,0:T(8,128)} all-gather(f32[128,256]{1,0:T(8,128)S(1)} %fusion.56), channel_id=6, replica_groups=mesh['sib'=4,'wide'=8] {'sib'}, dimensions={0}, use_global_device_ids=true | all-gather | bytes 655360 | tf_op jit(solution)/shard_map/all_gather | solution.py:82
  35.0 1.0 fusion.79
  35.9 0.9 fusion.75
  36.9 0.9 fusion.71
  37.8 2.6 %fusion.40 = f32[128,512]{1,0:T(8,128)} fusion(f32[1,1,512,512]{3,2,1,0:T(8,128)} %param.18, f32[128,1,512]{2,1,0:T(1,128)S(1)} %copy-done.11), kind=kOutput, calls=%fused_computation.73 | convolution fusion | flops 402653184 | bytes 1572864 | tf_op jit(solution)/shard_map/dot_general | solution.py:29
  40.5 2.5 convolution_add_fusion.5
  47.9 3.5 %collective-permute-start = (f32[1,32,256]{2,1,0:T(8,128)}, f32[1,32,256]{2,1,0:T(8,128)}, u32[]{:S(2)}, u32[]{:S(2)}) collective-permute-start(f32[1,32,256]{2,1,0:T(8,128)} %bitcast.227), channel_id=1, source_target_pairs={{0,7},{1,0},{2,1},{3,2},{4,3},{5,4},{6,5},{7,6},{8,15},{9,8},{10,9... | collective-permute-start | bytes 98312 | tf_op jit(solution)/shard_map/ppermute | solution.py:22
  51.5 1.2 collective-permute-done.1
  52.7 12.5 %reduce-scatter.5.cloned.1.call-done = f32[32,256]{1,0:T(8,128)} async-done(((f32[128,256]{1,0:T(8,128)}), f32[32,256]{1,0:T(8,128)}) %reduce-scatter.5.cloned.1.call-update) | async-done | bytes 32784 | tf_op jit(solution)/shard_map/reduce_scatter | solution.py:94
  65.2 14.6 %all-gather.1 = f32[256,256]{1,0:T(8,128)S(1)} all-gather(f32[32,256]{1,0:T(8,128)} %reduce-scatter.5.cloned.1.call-done), channel_id=3, replica_groups=mesh['sib'=4,'wide'=8] {'wide'}, dimensions={0}, use_global_device_ids=true | all-gather | bytes 294912 | tf_op jit(solution)/shard_map/all_gather | solution.py:97
  79.7 3.3 %collective-permute-start.2 = (f32[1,32,256]{2,1,0:T(8,128)}, f32[1,32,256]{2,1,0:T(8,128)S(1)}, u32[]{:S(2)}, u32[]{:S(2)}) collective-permute-start(f32[1,32,256]{2,1,0:T(8,128)} %collective-permute-done), channel_id=1, source_target_pairs={{0,7},{1,0},{2,1},{3,2},{4,3},{5,4},{6,5},{7,6},{8,15},{9,8},{10,9... | collective-permute-start | bytes 98312 | tf_op jit(solution)/shard_map/ppermute | solution.py:22
  83.0 1.1 fusion.115
  84.9 3.4 %collective-permute-start.4 = (f32[1,32,256]{2,1,0:T(8,128)S(1)}, f32[1,32,256]{2,1,0:T(8,128)S(1)}, u32[]{:S(2)}, u32[]{:S(2)}) collective-permute-start(f32[1,32,256]{2,1,0:T(8,128)S(1)} %collective-permute-done.2), channel_id=1, source_target_pairs={{0,7},{1,0},{2,1},{3,2},{4,3},{5,4},{6,5},{7,6},{8,15},{9,8},{10,9... | collective-permute-start | bytes 98312 | tf_op jit(solution)/shard_map/ppermute | solution.py:22
  88.7 1.8 convolution_bitcast_fusion.3
  90.5 3.3 %collective-permute-done.6 = f32[1,32,256]{2,1,0:T(8,128)S(1)} collective-permute-done((f32[1,32,256]{2,1,0:T(8,128)S(1)}, f32[1,32,256]{2,1,0:T(8,128)S(1)}, u32[]{:S(2)}, u32[]{:S(2)}) %collective-permute-start.6) | collective-permute-done | bytes 32800 | tf_op jit(solution)/shard_map/ppermute | solution.py:20
  94.4 1.4 fusion.35
  95.9 8.5 %all_gather.41 = f32[128,256]{1,0:T(8,128)S(1)} all-gather(f32[32,256]{1,0:T(8,128)S(1)} %fusion.35), channel_id=1, replica_groups=mesh['sib'=4,'wide'=8] {'sib'}, dimensions={0}, use_global_device_ids=true | all-gather | bytes 163840 | tf_op jit(solution)/shard_map/all_gather | solution.py:125
  108.2 1.8 copy.23
  112.5 0.9 fusion.31
  113.4 1.4 fusion.50
  114.8 14.8 %reduce-scatter.11.cloned.1.call-done = f32[32,256]{1,0:T(8,128)} async-done(((f32[128,256]{1,0:T(8,128)}), f32[32,256]{1,0:T(8,128)}) %reduce-scatter.11.cloned.1.call-update) | async-done | bytes 32784 | tf_op jit(solution)/shard_map/reduce_scatter | solution.py:95
  129.7 1.8 convolution_bitcast_fusion.5
  131.5 8.7 %all_gather.36 = f32[128,256]{1,0:T(8,128)S(1)} all-gather(f32[32,256]{1,0:T(8,128)S(1)} %convolution_bitcast_fusion.5), channel_id=1, replica_groups=mesh['sib'=4,'wide'=8] {'sib'}, dimensions={0}, use_global_device_ids=true | all-gather | bytes 163840 | tf_op jit(solution)/shard_map/all_gather | solution.py:124
  140.2 1.5 collective-permute-start.7
  142.3 1.0 collective-permute-done.7
  143.2 3.5 %collective-permute-start.9 = (f32[1,32,256]{2,1,0:T(8,128)S(1)}, f32[1,32,256]{2,1,0:T(8,128)}, u32[]{:S(2)}, u32[]{:S(2)}) collective-permute-start(f32[1,32,256]{2,1,0:T(8,128)S(1)} %collective-permute-done.7), channel_id=1, source_target_pairs={{0,7},{1,0},{2,1},{3,2},{4,3},{5,4},{6,5},{7,6},{8,15},{9,8},{10,9... | collective-permute-start | bytes 98312 | tf_op jit(solution)/shard_map/ppermute | solution.py:22
  146.8 13.7 %all-gather.5 = f32[512,256]{1,0:T(8,128)} all-gather(f32[128,256]{1,0:T(8,128)S(1)} %copy-done.20), channel_id=7, replica_groups=mesh['sib'=4,'wide'=8] {'sib'}, dimensions={0}, use_global_device_ids=true | all-gather | bytes 655360 | tf_op jit(solution)/shard_map/all_gather | solution.py:82
  160.5 1.6 collective-permute-start.11
  162.1 2.3 gather_fusion
  165.3 1.7 fusion.13
  168.4 10.5 %all-gather.2 = f32[512,256]{1,0:T(8,128)S(1)} all-gather(f32[128,256]{1,0:T(8,128)S(1)} %fusion.59), channel_id=4, replica_groups=mesh['sib'=4,'wide'=8] {'sib'}, dimensions={0}, use_global_device_ids=true | all-gather | bytes 655360 | tf_op jit(solution)/shard_map/all_gather | solution.py:81
  178.9 2.1 fusion.81
  181.0 0.9 fusion.77
  181.9 0.9 fusion.73
  182.9 0.9 fusion.69
  184.9 1.4 convolution_add_fusion.4
  190.6 0.9 fusion.15
  191.5 1.4 fusion.48
  193.0 15.9 %reduce-scatter.7.cloned.1.call-done = f32[32,256]{1,0:T(8,128)} async-done(((f32[128,256]{1,0:T(8,128)}), f32[32,256]{1,0:T(8,128)}) %reduce-scatter.7.cloned.1.call-update) | async-done | bytes 32784 | tf_op jit(solution)/shard_map/reduce_scatter | solution.py:94
  208.9 14.5 %all-gather.3 = f32[256,256]{1,0:T(8,128)S(1)} all-gather(f32[32,256]{1,0:T(8,128)} %reduce-scatter.7.cloned.1.call-done), channel_id=5, replica_groups=mesh['sib'=4,'wide'=8] {'wide'}, dimensions={0}, use_global_device_ids=true | all-gather | bytes 294912 | tf_op jit(solution)/shard_map/all_gather | solution.py:97
  223.8 1.8 convolution_bitcast_fusion.1
  226.9 1.5 fusion.34
  228.4 8.5 %all_gather.43 = f32[128,256]{1,0:T(8,128)S(1)} all-gather(f32[32,256]{1,0:T(8,128)S(1)} %fusion.34), channel_id=1, replica_groups=mesh['sib'=4,'wide'=8] {'sib'}, dimensions={0}, use_global_device_ids=true | all-gather | bytes 163840 | tf_op jit(solution)/shard_map/all_gather | solution.py:125
  238.5 1.0 copy.30
  239.5 7.5 %all_gather.39 = f32[128,256]{1,0:T(8,128)S(1)} all-gather(f32[32,256]{1,0:T(8,128)S(1)} %convolution_bitcast_fusion.4), channel_id=1, replica_groups=mesh['sib'=4,'wide'=8] {'sib'}, dimensions={0}, use_global_device_ids=true | all-gather | bytes 163840 | tf_op jit(solution)/shard_map/all_gather | solution.py:124
  248.8 1.0 copy.29
  (193 shorter events, 29.2 us)
Async XLA Ops:
  7.2 33.3 %copy-start = (f32[1,1,512,512]{3,2,1,0:T(8,128)S(1)}, f32[1,1,512,512]{3,2,1,0:T(8,128)}, u32[]{:S(2)}) copy-start(f32[1,1,512,512]{3,2,1,0:T(8,128)} %param.17) | copy-start | bytes 3145732
  7.2 1.7 copy-start.3
  7.2 40.1 %reduce-scatter.9.cloned.1.call-start = ((), (), s32[]{:S(2)}) async-start(), calls=%async_computation.7 | async-start | bytes 163840 | tf_op jit(solution)/shard_map/reduce_scatter | solution.py:95
  7.2 2.7 %copy-start.11 = (f32[128,1,512]{2,1,0:T(1,128)S(1)}, f32[128,1,512]{2,1,0:T(1,128)}, u32[]{:S(2)}) copy-start(f32[128,1,512]{2,1,0:T(1,128)} %param.15) | copy-start | bytes 786436
  8.9 1.0 copy-start.1
  9.9 55.3 %reduce-scatter.5.cloned.1.call-start = ((), (), s32[]{:S(2)}) async-start(), calls=%async_computation.5 | async-start | bytes 163840 | tf_op jit(solution)/shard_map/reduce_scatter | solution.py:94
  12.0 117.7 %reduce-scatter.11.cloned.1.call-start = ((), (), s32[]{:S(2)}) async-start(), calls=%async_computation.8 | async-start | bytes 163840 | tf_op jit(solution)/shard_map/reduce_scatter | solution.py:95
  12.0 22.6 %copy-start.6 = (f32[1,1,3,256,256]{4,3,2,1,0:T(8,128)S(1)}, f32[1,1,3,256,256]{4,3,2,1,0:T(8,128)}, u32[]{:S(2)}) copy-start(f32[1,1,3,256,256]{4,3,2,1,0:T(8,128)} %param.22) | copy-start | bytes 2359300
  40.5 2.6 copy-start.2
  40.5 2.6 copy-start.16
  47.3 5.3 %collective-permute-start.1 = (f32[1,32,256]{2,1,0:T(8,128)}, f32[1,32,256]{2,1,0:T(8,128)S(1)}, u32[]{:S(2)}, u32[]{:S(2)}) collective-permute-start(f32[1,32,256]{2,1,0:T(8,128)} %bitcast.226), channel_id=1, source_target_pairs={{0,1},{1,2},{2,3},{3,4},{4,5},{5,6},{6,7},{7,0},{8,9},{9,10},{10,1... | collective-permute-start | bytes 98312 | tf_op jit(solution)/shard_map/ppermute | solution.py:20
  47.9 45.9 %copy-start.46 = (f32[4]{0:T(128)}, f32[4]{0:T(128)S(1)}, u32[]{:S(2)}) copy-start(f32[4]{0:T(128)S(1)} %get-tuple-element.9) | copy-start | bytes 52
  47.9 31.8 %collective-permute-start = (f32[1,32,256]{2,1,0:T(8,128)}, f32[1,32,256]{2,1,0:T(8,128)}, u32[]{:S(2)}, u32[]{:S(2)}) collective-permute-start(f32[1,32,256]{2,1,0:T(8,128)} %bitcast.227), channel_id=1, source_target_pairs={{0,7},{1,0},{2,1},{3,2},{4,3},{5,4},{6,5},{7,6},{8,15},{9,8},{10,9... | collective-permute-start | bytes 98312 | tf_op jit(solution)/shard_map/ppermute | solution.py:22
  52.7 27.1 %copy-start.43 = (f32[1,32,256]{2,1,0:T(8,128)}, f32[1,32,256]{2,1,0:T(8,128)S(1)}, u32[]{:S(2)}) copy-start(f32[1,32,256]{2,1,0:T(8,128)S(1)} %collective-permute-done.1) | copy-start | bytes 98308
  52.7 30.4 %collective-permute-start.3 = (f32[1,32,256]{2,1,0:T(8,128)S(1)}, f32[1,32,256]{2,1,0:T(8,128)}, u32[]{:S(2)}, u32[]{:S(2)}) collective-permute-start(f32[1,32,256]{2,1,0:T(8,128)S(1)} %collective-permute-done.1), channel_id=1, source_target_pairs={{0,1},{1,2},{2,3},{3,4},{4,5},{5,6},{6,7},{7,0},{8,9},{9,10},{10,1... | collective-permute-start | bytes 98312 | tf_op jit(solution)/shard_map/ppermute | solution.py:20
  65.2 28.6 %copy-start.4 = (f32[1,4,256,256]{3,2,1,0:T(8,128)S(1)}, f32[1,4,256,256]{3,2,1,0:T(8,128)}, u32[]{:S(2)}) copy-start(f32[1,4,256,256]{3,2,1,0:T(8,128)} %param.24) | copy-start | bytes 3145732
  79.7 5.2 %collective-permute-start.2 = (f32[1,32,256]{2,1,0:T(8,128)}, f32[1,32,256]{2,1,0:T(8,128)S(1)}, u32[]{:S(2)}, u32[]{:S(2)}) collective-permute-start(f32[1,32,256]{2,1,0:T(8,128)} %collective-permute-done), channel_id=1, source_target_pairs={{0,7},{1,0},{2,1},{3,2},{4,3},{5,4},{6,5},{7,6},{8,15},{9,8},{10,9... | collective-permute-start | bytes 98312 | tf_op jit(solution)/shard_map/ppermute | solution.py:22
  83.0 5.6 %collective-permute-start.5 = (f32[1,32,256]{2,1,0:T(8,128)}, f32[1,32,256]{2,1,0:T(8,128)S(1)}, u32[]{:S(2)}, u32[]{:S(2)}) collective-permute-start(f32[1,32,256]{2,1,0:T(8,128)} %collective-permute-done.3), channel_id=1, source_target_pairs={{0,1},{1,2},{2,3},{3,4},{4,5},{5,6},{6,7},{7,0},{8,9},{9,10},{10,1... | collective-permute-start | bytes 98312 | tf_op jit(solution)/shard_map/ppermute | solution.py:20
  84.9 5.5 %collective-permute-start.4 = (f32[1,32,256]{2,1,0:T(8,128)S(1)}, f32[1,32,256]{2,1,0:T(8,128)S(1)}, u32[]{:S(2)}, u32[]{:S(2)}) collective-permute-start(f32[1,32,256]{2,1,0:T(8,128)S(1)} %collective-permute-done.2), channel_id=1, source_target_pairs={{0,7},{1,0},{2,1},{3,2},{4,3},{5,4},{6,5},{7,6},{8,15},{9,8},{10,9... | collective-permute-start | bytes 98312 | tf_op jit(solution)/shard_map/ppermute | solution.py:22
  88.6 5.1 %collective-permute-start.6 = (f32[1,32,256]{2,1,0:T(8,128)S(1)}, f32[1,32,256]{2,1,0:T(8,128)S(1)}, u32[]{:S(2)}, u32[]{:S(2)}) collective-permute-start(f32[1,32,256]{2,1,0:T(8,128)S(1)} %collective-permute-done.5), channel_id=1, source_target_pairs={{0,1},{1,2},{2,3},{3,4},{4,5},{5,6},{6,7},{7,0},{8,9},{9,10},{10,1... | collective-permute-start | bytes 98312 | tf_op jit(solution)/shard_map/ppermute | solution.py:20
  88.6 5.2 %copy-start.34 = (f32[32,256]{1,0:T(8,128)S(1)}, f32[32,256]{1,0:T(8,128)}, u32[]{:S(2)}) copy-start(f32[32,256]{1,0:T(8,128)} %reduce-scatter.9.cloned.1.call-done) | copy-start | bytes 98308
  88.7 5.2 %copy-start.44 = (f32[1,32,256]{2,1,0:T(8,128)S(1)}, f32[1,32,256]{2,1,0:T(8,128)}, u32[]{:S(2)}) copy-start(f32[1,32,256]{2,1,0:T(8,128)} %copy-done.43) | copy-start | bytes 98308
  95.9 8.6 %copy-start.26 = (f32[128,256]{1,0:T(8,128)S(1)}, f32[128,256]{1,0:T(8,128)}, u32[]{:S(2)}) copy-start(f32[128,256]{1,0:T(8,128)} %fusion.22) | copy-start | bytes 393220
  104.5 1.0 copy-start.21
  108.1 54.0 %all-gather.8.cloned.1.call-start = ((), (), s32[]{:S(2)}) async-start(), calls=%async_computation.4 | async-start | bytes 1310720 | tf_op jit(solution)/shard_map/all_gather | solution.py:65
  110.0 98.8 %reduce-scatter.7.cloned.1.call-start = ((), (), s32[]{:S(2)}) async-start(), calls=%async_computation.6 | async-start | bytes 163840 | tf_op jit(solution)/shard_map/reduce_scatter | solution.py:94
  129.7 12.0 %collective-permute-start.8 = (f32[1,32,256]{2,1,0:T(8,128)}, f32[1,32,256]{2,1,0:T(8,128)S(1)}, u32[]{:S(2)}, u32[]{:S(2)}) collective-permute-start(f32[1,32,256]{2,1,0:T(8,128)} %bitcast.228), channel_id=1, source_target_pairs={{0,1},{1,2},{2,3},{3,4},{4,5},{5,6},{6,7},{7,0},{8,9},{9,10},{10,1... | collective-permute-start | bytes 98312 | tf_op jit(solution)/shard_map/ppermute | solution.py:20
  131.5 8.7 %copy-start.35 = (f32[32,256]{1,0:T(8,128)S(1)}, f32[32,256]{1,0:T(8,128)}, u32[]{:S(2)}) copy-start(f32[32,256]{1,0:T(8,128)} %reduce-scatter.11.cloned.1.call-done) | copy-start | bytes 98308
  131.5 10.1 %copy-start.24 = (f32[128,256]{1,0:T(8,128)S(1)}, f32[128,256]{1,0:T(8,128)}, u32[]{:S(2)}) copy-start(f32[128,256]{1,0:T(8,128)} %fusion.31) | copy-start | bytes 393220
  140.2 6.6 %copy-start.20 = (f32[128,256]{1,0:T(8,128)S(1)}, f32[128,256]{1,0:T(8,128)}, u32[]{:S(2)}) copy-start(f32[128,256]{1,0:T(8,128)} %copy-done.19) | copy-start | bytes 393220
  140.2 3.1 %collective-permute-start.7 = (f32[1,32,256]{2,1,0:T(8,128)S(1)}, f32[1,32,256]{2,1,0:T(8,128)S(1)}, u32[]{:S(2)}, u32[]{:S(2)}) collective-permute-start(f32[1,32,256]{2,1,0:T(8,128)S(1)} %bitcast.229), channel_id=1, source_target_pairs={{0,7},{1,0},{2,1},{3,2},{4,3},{5,4},{6,5},{7,6},{8,15},{9,8},{10,9... | collective-permute-start | bytes 98312 | tf_op jit(solution)/shard_map/ppermute | solution.py:22
  141.6 5.1 %collective-permute-start.10 = (f32[1,32,256]{2,1,0:T(8,128)S(1)}, f32[1,32,256]{2,1,0:T(8,128)S(1)}, u32[]{:S(2)}, u32[]{:S(2)}) collective-permute-start(f32[1,32,256]{2,1,0:T(8,128)S(1)} %collective-permute-done.8), channel_id=1, source_target_pairs={{0,1},{1,2},{2,3},{3,4},{4,5},{5,6},{6,7},{7,0},{8,9},{9,10},{10,1... | collective-permute-start | bytes 98312 | tf_op jit(solution)/shard_map/ppermute | solution.py:20
  143.2 17.2 %copy-start.39 = (f32[1,32,256]{2,1,0:T(8,128)}, f32[1,32,256]{2,1,0:T(8,128)S(1)}, u32[]{:S(2)}) copy-start(f32[1,32,256]{2,1,0:T(8,128)S(1)} %collective-permute-done.7) | copy-start | bytes 98308
  143.2 17.2 %collective-permute-start.9 = (f32[1,32,256]{2,1,0:T(8,128)S(1)}, f32[1,32,256]{2,1,0:T(8,128)}, u32[]{:S(2)}, u32[]{:S(2)}) collective-permute-start(f32[1,32,256]{2,1,0:T(8,128)S(1)} %collective-permute-done.7), channel_id=1, source_target_pairs={{0,7},{1,0},{2,1},{3,2},{4,3},{5,4},{6,5},{7,6},{8,15},{9,8},{10,9... | collective-permute-start | bytes 98312 | tf_op jit(solution)/shard_map/ppermute | solution.py:22
  146.8 13.7 %copy-start.41 = (f32[1,32,256]{2,1,0:T(8,128)}, f32[1,32,256]{2,1,0:T(8,128)S(1)}, u32[]{:S(2)}) copy-start(f32[1,32,256]{2,1,0:T(8,128)S(1)} %collective-permute-done.10) | copy-start | bytes 98308
  146.8 15.3 %collective-permute-start.12 = (f32[1,32,256]{2,1,0:T(8,128)S(1)}, f32[1,32,256]{2,1,0:T(8,128)}, u32[]{:S(2)}, u32[]{:S(2)}) collective-permute-start(f32[1,32,256]{2,1,0:T(8,128)S(1)} %collective-permute-done.10), channel_id=1, source_target_pairs={{0,1},{1,2},{2,3},{3,4},{4,5},{5,6},{6,7},{7,0},{8,9},{9,10},{10,1... | collective-permute-start | bytes 98312 | tf_op jit(solution)/shard_map/ppermute | solution.py:20
  160.5 65.8 %collective-permute-start.11 = (f32[1,32,256]{2,1,0:T(8,128)}, f32[1,32,256]{2,1,0:T(8,128)}, u32[]{:S(2)}, u32[]{:S(2)}) collective-permute-start(f32[1,32,256]{2,1,0:T(8,128)} %collective-permute-done.9), channel_id=1, source_target_pairs={{0,7},{1,0},{2,1},{3,2},{4,3},{5,4},{6,5},{7,6},{8,15},{9,8},{10,9... | collective-permute-start | bytes 98312 | tf_op jit(solution)/shard_map/ppermute | solution.py:22
  162.1 64.2 %collective-permute-start.13 = (f32[1,32,256]{2,1,0:T(8,128)}, f32[1,32,256]{2,1,0:T(8,128)}, u32[]{:S(2)}, u32[]{:S(2)}) collective-permute-start(f32[1,32,256]{2,1,0:T(8,128)} %collective-permute-done.12), channel_id=1, source_target_pairs={{0,1},{1,2},{2,3},{3,4},{4,5},{5,6},{6,7},{7,0},{8,9},{9,10},{10,1... | collective-permute-start | bytes 98312 | tf_op jit(solution)/shard_map/ppermute | solution.py:20
  168.4 12.6 %copy-start.7 = (f32[1,1,3,256,256]{4,3,2,1,0:T(8,128)S(1)}, f32[1,1,3,256,256]{4,3,2,1,0:T(8,128)}, u32[]{:S(2)}) copy-start(f32[1,1,3,256,256]{4,3,2,1,0:T(8,128)} %param.22) | copy-start | bytes 2359300
  178.9 5.7 %copy-start.8 = (f32[512,256]{1,0:T(8,128)}, f32[512,256]{1,0:T(8,128)S(1)}, u32[]{:S(2)}) copy-start(f32[512,256]{1,0:T(8,128)S(1)} %all-gather.2) | copy-start | bytes 1572868
  178.9 5.0 %copy-start.10 = (f32[1,1,512,512]{3,2,1,0:T(8,128)S(1)}, f32[1,1,512,512]{3,2,1,0:T(8,128)}, u32[]{:S(2)}) copy-start(f32[1,1,512,512]{3,2,1,0:T(8,128)} %param.18) | copy-start | bytes 3145732
  184.9 1.4 copy-start.9
  186.6 1.0 copy-start.17
  191.5 31.9 %copy-start.60 = (s32[1,4]{1,0:T(1,128)S(1)}, s32[1,4]{1,0:T(1,128)}, u32[]{:S(2)}) copy-start(s32[1,4]{1,0:T(1,128)} %param.23) | copy-start | bytes 52
  193.0 32.7 %copy-start.5 = (f32[1,4,256,256]{3,2,1,0:T(8,128)S(1)}, f32[1,4,256,256]{3,2,1,0:T(8,128)}, u32[]{:S(2)}) copy-start(f32[1,4,256,256]{3,2,1,0:T(8,128)} %param.24) | copy-start | bytes 3145732
  228.4 8.5 %copy-start.30 = (f32[128,256]{1,0:T(8,128)S(1)}, f32[128,256]{1,0:T(8,128)}, u32[]{:S(2)}) copy-start(f32[128,256]{1,0:T(8,128)} %fusion.15) | copy-start | bytes 393220
  247.0 1.0 copy-start.23
  247.1 1.0 copy-start.57
  (32 other events, 25.5 us)
Sparse Core Ops, SparseCore 0:
  10.7 26.8 reduce-scatter.8
  41.0 24.1 reduce-scatter.4
  108.3 21.3 reduce-scatter.10
  131.9 29.3 all-gather.7
  185.0 23.8 reduce-scatter.6
